TPU v7x, 32 devices: a whole 2x2x4 slice. The times are simulated.
32 devices in a mesh: site: 8 (over z, y), ka: 4 (over x, core).
Axes of the slice: x: 2, y: 2, z: 4, core: 2. Of those that a mesh axis runs over, the one named last changes fastest.
Arguments:
- positions: float32 [3, 128], P(None, 'site'), may hold values from 0 to 1
- site_class: int32 [128], P('site'), may hold values from 0 to 3
- class_charge: float32 [4], replicated, may hold values from -2 to 2
- miller: int32 [3, 524288], P(None, 'ka'), may hold values from -80 to 80, as said below
Outputs:
- forces: float32 [3, 128], P(None, ('site', 'ka'))
- energy: float32 [], replicated
Inputs may be any that keep to these rules, and one draw needn't show every extreme that they name: `miller`: the k-vectors are all distinct, and none has all three indices zero.
All inputs are finite; a program needn't handle non-finite values.
Results may differ from a plain program's by a relative error of at most 0.0003.
Values sent between devices are 32-bit elements; how exact they have to be, the bound alone decides.
A program may use at most 64 MiB of HBM per device.

v0:
```python
import functools
import math

import jax
import jax.numpy as jnp
from jax import lax
from jax.experimental import pallas as pl
from jax.experimental.pallas import tpu as pltpu
from jax.sharding import PartitionSpec as P

MMAX = 80
NCLS = 4
MESH = pl.DeviceIdType.MESH
F32 = jnp.float32
BF16 = jnp.bfloat16
A0, A1, A2 = 1.5707884689227576, -0.645711988911062, 0.07766738858001387
TINY = 1e-24
KB = 512
ROWS = 16


def kernel(
    nsite, nka, nsites, kvecs,
    pos_ref, cls_ref, cc_ref, mil_ref,
    out_ref, en_ref,
    mi, m16, wts, x16, alpha2, ca0, ca1, ca2, qabs, sh, ch, vbuf, facc, eacc, qtot, tbuf, gr1, gr2,
    ag_out, ag_in, rs_out, rs_in,
    mil_sem, ag_send, ag_recv, rs_send, rs_recv,
):
    ndev = nsite * nka
    si, ki = lax.axis_index("site"), lax.axis_index("ka")
    me = si * nka + ki
    ls = pos_ref.shape[1]
    sub = mi.shape[1]
    spd = nsites // ndev
    nblk = sub // KB

    mil_copy = pltpu.make_async_copy(
        mil_ref.at[:, pl.ds(pl.multiple_of(si * sub, 128), sub)], mi, mil_sem
    )
    mil_copy.start()

    cls = cls_ref[...]
    charge = jnp.zeros(cls.shape, F32)
    for c in range(NCLS):
        charge = jnp.where(cls == c, cc_ref[c], charge)
    ag_out[...] = jnp.zeros_like(ag_out)
    ag_out[0:3, 0:ls] = pos_ref[...]
    ag_out[3:4, 0:ls] = charge

    barrier = pltpu.get_barrier_semaphore()

    @pl.loop(1, ndev)
    def _(i):
        to = lax.rem(me + i, ndev)
        pl.semaphore_signal(
            barrier, inc=1, device_id=(lax.div(to, nka), lax.rem(to, nka)), device_id_type=MESH
        )

    mil_copy.wait()

    @pl.loop(0, nblk)
    def _(b):
        at = pl.ds(pl.multiple_of(b * KB, KB), KB)
        m = mi[:, at].astype(F32)
        sq = jnp.sum(m * m, axis=0, keepdims=True)
        limit = float(MMAX * MMAX)
        wts[:, at] = limit * jnp.exp(sq * (-1.0 / limit)) / sq
        m16[:, at] = jnp.concatenate(
            [m, m, m, jnp.ones((1, KB), F32), jnp.zeros((6, KB), F32)], axis=0
        ).astype(BF16)

    pl.semaphore_wait(barrier, ndev - 1)

    def ag_copy(src, to):
        return pltpu.make_async_remote_copy(
            src_ref=ag_out, dst_ref=ag_in.at[src], send_sem=ag_send.at[to],
            recv_sem=ag_recv.at[src], device_id=(to, ki), device_id_type=MESH,
        )

    @pl.loop(1, nsite)
    def _(i):
        ag_copy(si, lax.rem(si + i, nsite)).start()

    ag_in[si] = ag_out[...]

    @pl.loop(1, nsite)
    def _(i):
        other = lax.rem(si + i, nsite)
        ag_copy(other, other).wait_recv()

    per = 128 // ls
    for t in range(nsites // 128):
        allrows = ag_in[t * per]
        for i in range(1, per):
            allrows = allrows + pltpu.roll(ag_in[t * per + i], i * ls, 1)
        x = allrows[0:3]
        x = x - jnp.round(x)
        q = allrows[3:4]
        x1 = x.astype(BF16).astype(F32)
        x2 = (x - x1).astype(BF16).astype(F32)
        x3 = x - x1 - x2
        half = jnp.where(q < 0.0, 0.5, 0.0)
        qc = jnp.maximum(jnp.abs(q), TINY)
        al2 = jnp.sqrt(qc)
        al = jnp.sqrt(al2)
        rows = jnp.concatenate(
            [x1, x2, x3, half, al2, al * A0, al * A1, al * A2, jnp.abs(q), qc,
             jnp.zeros((112, 128), F32)], axis=0
        )
        cols = rows.T
        rs_ = pl.ds(t * 128, 128)
        x16[rs_, :] = cols[:, 0:16].astype(BF16)
        alpha2[rs_, :] = jnp.broadcast_to(cols[:, 10:11], (128, 128))
        ca0[rs_, :] = jnp.broadcast_to(cols[:, 11:12], (128, 128))
        ca1[rs_, :] = jnp.broadcast_to(cols[:, 12:13], (128, 128))
        ca2[rs_, :] = jnp.broadcast_to(cols[:, 13:14], (128, 128))
        qabs[rs_, 0:2] = cols[:, 14:16]
        total = jnp.broadcast_to(jnp.sum(qc, axis=1, keepdims=True), (1, 128))
        qtot[...] = total if t == 0 else qtot[...] + total

    facc[...] = jnp.zeros_like(facc)
    eacc[...] = jnp.zeros_like(eacc)
    isn = 1.0 / math.sqrt(nsites)

    def wide(v):
        return jnp.concatenate([v] * (KB // 128), axis=1)

    def cols_of(b):
        return pl.ds(pl.multiple_of(b * KB, KB), KB)

    def split(v, rows):
        hi = v.astype(BF16)
        vbuf[rows, 0:KB] = hi
        vbuf[rows, KB:] = (v - hi.astype(F32)).astype(BF16)

    def gather_forces(b):
        mb = m16[:, cols_of(b)]
        facc[...] += lax.dot_general(
            vbuf[...], jnp.concatenate([mb, mb], axis=1), (((1,), (1,)), ((), ())),
            preferred_element_type=F32,
        )

    def second(rr):
        split(sh[rr] * gr1[...] + ch[rr] * gr2[...], rr)

    extra = slice(nsites, nsites + ROWS)
    chunks = [slice(j * ROWS, (j + 1) * ROWS) for j in range(nsites // ROWS)]
    for buf in (sh, ch, gr1, gr2, vbuf):
        buf[...] = jnp.zeros_like(buf)
    tbuf[...] = jnp.dot(x16[...], m16[:, 0:KB], preferred_element_type=F32)

    @pl.loop(0, nblk)
    def _(b):
        gather_forces(jnp.maximum(b - 2, 0))
        turns = jnp.dot(
            x16[...], m16[:, cols_of(jnp.minimum(b + 1, nblk - 1))], preferred_element_type=F32
        )
        sums = sumc = None
        for j, rr in enumerate(chunks):
            second(rr)
            t = tbuf[rr]
            r = t - jnp.round(t)
            z = r * r
            s = r * (wide(ca0[rr]) + z * (wide(ca1[rr]) + z * wide(ca2[rr])))
            s2 = s * s
            u = wide(alpha2[rr]) - s2
            sc = s * (u * lax.rsqrt(u))
            dc = u - s2
            sj = sc * dc
            cj = sc * sc
            sh[rr] = sj
            ch[rr] = cj
            tbuf[rr] = turns[rr]
            sums = sj if j == 0 else sums + sj
            sumc = cj if j == 0 else sumc + cj
        split(jnp.broadcast_to(gr2[...], (ROWS, KB)), extra)
        cimag = (4.0 * isn) * jnp.sum(sums, axis=0, keepdims=True)
        creal = isn * (wide(qtot[...]) - 8.0 * jnp.sum(sumc, axis=0, keepdims=True))
        w = wts[:, cols_of(b)]
        g1 = w * creal
        g2 = w * cimag
        eacc[...] += g1 * creal + g2 * cimag
        gr1[...] = g1
        gr2[...] = 2.0 * g2

    gather_forces(max(nblk - 2, 0))
    for rr in chunks:
        second(rr)
    split(jnp.broadcast_to(gr2[...], (ROWS, KB)), extra)
    gather_forces(nblk - 1)

    energy = jnp.sum(eacc[...], axis=1, keepdims=True) * (1.0 / kvecs)
    fscale = 4.0 * math.pi / math.sqrt(nsites * kvecs)
    qa, qc = qabs[:, 0:1], qabs[:, 1:2]
    forces = (fscale * (qa / qc)) * (4.0 * facc[0:nsites] - (0.5 * qc) * facc[nsites : nsites + 1])
    lane = lax.broadcasted_iota(jnp.int32, forces.shape, 1)
    forces = jnp.where(lane == 3, energy, forces)
    rs_out[...] = jnp.zeros_like(rs_out)
    for p in range(ndev):
        rs_out[p, :, 0:16] = forces[p * spd : (p + 1) * spd]

    def rs_copy(src, to):
        return pltpu.make_async_remote_copy(
            src_ref=rs_out.at[to], dst_ref=rs_in.at[src], send_sem=rs_send.at[to],
            recv_sem=rs_recv.at[src], device_id=(lax.div(to, nka), lax.rem(to, nka)),
            device_id_type=MESH,
        )

    @pl.loop(1, ndev)
    def _(i):
        rs_copy(me, lax.rem(me + i, ndev)).start()

    rs_in[me] = rs_out[me]

    @pl.loop(1, ndev)
    def _(i):
        other = lax.rem(me + i, ndev)
        rs_copy(other, me).wait_recv()

    mine = jnp.sum(rs_in[...], axis=0)
    sub_i = lax.broadcasted_iota(jnp.int32, (spd, 128), 0)
    lane_i = lax.broadcasted_iota(jnp.int32, (spd, 128), 1)
    for d in range(3):
        row = jnp.sum(jnp.where(sub_i == lane_i, mine[:, d : d + 1], 0.0), axis=0, keepdims=True)
        out_ref[d : d + 1, :] = row[:, 0:spd]
    en_ref[...] = mine[0:1, 3:4]

    @pl.loop(1, ndev)
    def _(i):
        rs_copy(me, lax.rem(me + i, ndev)).wait_send()

    @pl.loop(1, nsite)
    def _(i):
        ag_copy(si, lax.rem(si + i, nsite)).wait_send()


def local(nsite, nka, positions, site_class, class_charge, miller):
    ndev = nsite * nka
    ls = positions.shape[1]
    nsites = ls * nsite
    kvecs = miller.shape[1] * nka
    sub = miller.shape[1] // nsite
    spd = nsites // ndev
    vmem = pl.BlockSpec(memory_space=pltpu.VMEM)
    forces, energy = pl.pallas_call(
        functools.partial(kernel, nsite, nka, nsites, kvecs),
        out_shape=(jax.ShapeDtypeStruct((3, spd), F32), jax.ShapeDtypeStruct((1, 1), F32)),
        in_specs=[
            vmem, vmem, pl.BlockSpec(memory_space=pltpu.SMEM), pl.BlockSpec(memory_space=pl.ANY),
        ],
        out_specs=(vmem, vmem),
        scratch_shapes=[
            pltpu.VMEM((3, sub), jnp.int32),
            pltpu.VMEM((16, sub), BF16),
            pltpu.VMEM((1, sub), F32),
            pltpu.VMEM((nsites, 16), BF16),
            pltpu.VMEM((nsites, 128), F32),
            pltpu.VMEM((nsites, 128), F32),
            pltpu.VMEM((nsites, 128), F32),
            pltpu.VMEM((nsites, 128), F32),
            pltpu.VMEM((nsites, 128), F32),
            pltpu.VMEM((nsites, KB), F32),
            pltpu.VMEM((nsites, KB), F32),
            pltpu.VMEM((nsites + ROWS, 2 * KB), BF16),
            pltpu.VMEM((nsites + ROWS, 16), F32),
            pltpu.VMEM((1, KB), F32),
            pltpu.VMEM((1, 128), F32),
            pltpu.VMEM((nsites, KB), F32),
            pltpu.VMEM((1, KB), F32),
            pltpu.VMEM((1, KB), F32),
            pltpu.VMEM((8, 128), F32),
            pltpu.VMEM((nsite, 8, 128), F32),
            pltpu.VMEM((ndev, spd, 128), F32),
            pltpu.VMEM((ndev, spd, 128), F32),
            pltpu.SemaphoreType.DMA,
            pltpu.SemaphoreType.DMA((nsite,)),
            pltpu.SemaphoreType.DMA((nsite,)),
            pltpu.SemaphoreType.DMA((ndev,)),
            pltpu.SemaphoreType.DMA((ndev,)),
        ],
        compiler_params=pltpu.CompilerParams(collective_id=0, has_side_effects=True),
        name="ewald",
    )(positions, site_class.reshape(1, ls), class_charge, miller)
    return forces, energy[0, 0]


def solution(mesh):
    placed = (P(None, "site"), P("site"), P(), P(None, "ka"))
    return jax.shard_map(
        functools.partial(local, mesh.shape["site"], mesh.shape["ka"]),
        mesh=mesh,
        in_specs=placed,
        out_specs=(P(None, ("site", "ka")), P()),
        check_vma=False,
    )
```

profile of v0, /device:TPU:0, one launch (start us, length us, event | category | flops | bytes accessed | tf_op | source)
XLA Modules:
  0.0 33.1 jit_solution(824961050059176871)
XLA Ops:
  0.6 29.5 %ewald.1 = (f32[3,4]{1,0:T(4,128)}, f32[1,1]{1,0:T(1,128)}) custom-call(f32[3,16]{1,0:T(4,128)} %pos_ref.1, s32[1,16]{1,0:T(1,128)} %bitcast.2, f32[4]{0:T(128)} %cc_ref.1, s32[3,131072]{1,0:T(4,128)} %mil_ref.1), custom_call_target="tpu_custom_call" | custom-call | tf_op jit(solution)/shard_map/ewald/pallas_call | solution.py:246
  30.1 1.2 %copy.8 = f32[3,4]{1,0:T(4,128)} copy(f32[3,4]{1,0:T(4,128)} %get-tuple-element.8) | data formatting | bytes 96
where the time goes:
time: 33.4 us; the launch traced here: 33.1 us
  Pallas kernels  29.5 us (88%)
  between operations  2.4 us (7%)
  local copies, waits for them, and re-layouts  1.25 us (4%)
    pallas_call x1, Pallas kernels, local(): pl.pallas_call(functools.partial(kernel, nsite, nka, nsites, kvecs), out_...  29.5 us
    unnamed x1, local copies, waits for them, and re-layouts  1.25 us

commit v1 on v0

--- a/solution.py
+++ b/solution.py
@@ -22,7 +22,7 @@
 def kernel(
     nsite, nka, nsites, kvecs,
     pos_ref, cls_ref, cc_ref, mil_ref,
-    out_ref, en_ref,
+    res_ref,
     mi, m16, wts, x16, alpha2, ca0, ca1, ca2, qabs, sh, ch, vbuf, facc, eacc, qtot, tbuf, gr1, gr2,
     ag_out, ag_in, rs_out, rs_in,
     mil_sem, ag_send, ag_recv, rs_send, rs_recv,
@@ -223,8 +223,9 @@
     lane_i = lax.broadcasted_iota(jnp.int32, (spd, 128), 1)
     for d in range(3):
         row = jnp.sum(jnp.where(sub_i == lane_i, mine[:, d : d + 1], 0.0), axis=0, keepdims=True)
-        out_ref[d : d + 1, :] = row[:, 0:spd]
-    en_ref[...] = mine[0:1, 3:4]
+        res_ref[d : d + 1, :] = row
+    res_ref[3:4, :] = jnp.broadcast_to(mine[0:1, 3:4], (1, 128))
+    res_ref[4:8, :] = jnp.zeros((4, 128), F32)
 
     @pl.loop(1, ndev)
     def _(i):
@@ -233,6 +234,11 @@
     @pl.loop(1, nsite)
     def _(i):
         ag_copy(si, lax.rem(si + i, nsite)).wait_send()
+
+
+def publish(res_ref, out_ref, en_ref):
+    out_ref[...] = res_ref[0:3, 0 : out_ref.shape[1]]
+    en_ref[...] = res_ref[3:4, 0:1]
 
 
 def local(nsite, nka, positions, site_class, class_charge, miller):
@@ -243,13 +249,13 @@
     sub = miller.shape[1] // nsite
     spd = nsites // ndev
     vmem = pl.BlockSpec(memory_space=pltpu.VMEM)
-    forces, energy = pl.pallas_call(
+    summed = pl.pallas_call(
         functools.partial(kernel, nsite, nka, nsites, kvecs),
-        out_shape=(jax.ShapeDtypeStruct((3, spd), F32), jax.ShapeDtypeStruct((1, 1), F32)),
+        out_shape=pltpu.VMEM((8, 128), F32),
         in_specs=[
             vmem, vmem, pl.BlockSpec(memory_space=pltpu.SMEM), pl.BlockSpec(memory_space=pl.ANY),
         ],
-        out_specs=(vmem, vmem),
+        out_specs=vmem,
         scratch_shapes=[
             pltpu.VMEM((3, sub), jnp.int32),
             pltpu.VMEM((16, sub), BF16),
@@ -282,6 +288,13 @@
         compiler_params=pltpu.CompilerParams(collective_id=0, has_side_effects=True),
         name="ewald",
     )(positions, site_class.reshape(1, ls), class_charge, miller)
+    forces, energy = pl.pallas_call(
+        publish,
+        out_shape=(jax.ShapeDtypeStruct((3, spd), F32), jax.ShapeDtypeStruct((1, 1), F32)),
+        in_specs=[vmem],
+        out_specs=(vmem, vmem),
+        name="publish",
+    )(pltpu.with_memory_space_constraint(summed, pltpu.VMEM))
     return forces, energy[0, 0]
 
 

time: 33.4 us -> 30.3 us (0.907)
  between operations: 2.4 us -> 0.64 us
  local copies, waits for them, and re-layouts: 1.25 us -> 0 us
    unnamed x1 -> x0, local copies, waits for them, and re-layouts: 1.25 us -> none
    pallas_call x1, Pallas kernels: 29.5 us -> 28.9 us  [local(): pl.pallas_call(functools.partial(kernel, nsite, nka, nsites, kvecs), out_...]
    pallas_call x0 -> x1, Pallas kernels: none -> 0.58 us  [local(): pl.pallas_call(publish, out_shape=(jax.ShapeDtypeStruct((3, spd), F32), j...]
where the time goes in v1:
time: 30.3 us; the launch traced here: 30.1 us
  Pallas kernels  29.5 us (97%)
  between operations  0.64 us (2%)
    pallas_call x1, Pallas kernels, local(): pl.pallas_call(functools.partial(kernel, nsite, nka, nsites, kvecs), out_...  28.9 us

profile of v1, /device:TPU:0, one launch (start us, length us, event | category | flops | bytes accessed | tf_op | source)
XLA Modules:
  0.0 30.1 jit_solution(4674749625864572292)
XLA Ops:
  0.6 28.9 %ewald.1.res_ref = f32[8,128]{1,0:T(8,128)S(1)} custom-call(f32[3,16]{1,0:T(4,128)} %pos_ref.1, s32[1,16]{1,0:T(1,128)} %bitcast.2, f32[4]{0:T(128)} %cc_ref.1, s32[3,131072]{1,0:T(4,128)} %mil_ref.1), custom_call_target="tpu_custom_call" | custom-call | tf_op jit(solution)/shard_map/ewald/pallas_call | solution.py:252
  29.5 0.6 %publish.1 = (f32[3,4]{1,0:T(4,128)}, f32[1,1]{1,0:T(1,128)}) custom-call(f32[8,128]{1,0:T(8,128)S(1)} %ewald.1.res_ref), custom_call_target="tpu_custom_call" | custom-call | tf_op jit(solution)/shard_map/publish/pallas_call | solution.py:291

commit v2 on v1

v2 whole, which is shorter than its diff:
```python
import functools
import math

import jax
import jax.numpy as jnp
from jax import lax
from jax.experimental import pallas as pl
from jax.experimental.pallas import tpu as pltpu
from jax.sharding import PartitionSpec as P

MMAX = 80
NCLS = 4
MESH = pl.DeviceIdType.MESH
F32 = jnp.float32
BF16 = jnp.bfloat16
A0, A1, A2 = 1.5707884689227576, -0.645711988911062, 0.07766738858001387
TINY = 1e-24
UNITS = 4
SKEW = (1, 0)
KBW = 1024


def shares(nsite, units):
    total, top = SKEW[0] * nsite, SKEW[1]
    span = nsite * (total - top * nsite)

    def first(s):
        return units * s * (total - top * s) // span

    return first, max(first(s + 1) - first(s) for s in range(nsite))


def kernel(
    nsite, nka, nsites, kvecs, kb,
    pos_ref, cls_ref, cc_ref, mil_ref,
    res_ref,
    posv, clsv, ccv, mi, m16, wts, pbuf, xs, co, tbuf, psin, pcos, ssin, scos,
    qrow, qtot, g1v, g2v, facc, eacc,
    ag_out, ag_in, rs_out, rs_in,
    pos_sem, cls_sem, cc_sem, mil_sem, ag_send, ag_recv, rs_send, rs_recv, ready, kin, kall,
):
    ndev = nsite * nka
    si, ki = lax.axis_index("site"), lax.axis_index("ka")
    me = si * nka + ki
    ls = posv.shape[1]
    spd = nsites // ndev
    units = mil_ref.shape[1] // kb
    first, most = shares(nsite, units)
    low = first(si)
    n = first(si + 1) - low
    base = jnp.minimum(low, units - most)
    shift = low - base

    pos_copy = pltpu.make_async_copy(pos_ref, posv, pos_sem)
    cls_copy = pltpu.make_async_copy(cls_ref, clsv, cls_sem)
    cc_copy = pltpu.make_async_copy(cc_ref, ccv, cc_sem)
    mil_copy = pltpu.make_async_copy(
        mil_ref.at[:, pl.ds(pl.multiple_of(base * kb, 128), most * kb)], mi, mil_sem
    )
    pos_copy.start()
    cls_copy.start()
    cc_copy.start()
    mil_copy.start()

    barrier = pltpu.get_barrier_semaphore()

    def tell(sem, s, k):
        pl.semaphore_signal(sem, inc=1, device_id=(s, k), device_id_type=MESH)

    @pl.loop(si + 1, nsite)
    def _(s):
        tell(barrier, s, ki)

    @pl.loop(ki + 1, nka)
    def _(k):
        tell(barrier, si, k)

    ssin[...] = jnp.zeros_like(ssin)
    scos[...] = jnp.zeros_like(scos)
    qrow[...] = jnp.zeros_like(qrow)
    qtot[...] = jnp.zeros_like(qtot)
    facc[...] = jnp.zeros_like(facc)
    eacc[...] = jnp.zeros_like(eacc)
    pbuf[...] = jnp.zeros_like(pbuf)

    pos_copy.wait()
    cls_copy.wait()
    cc_copy.wait()
    cls = clsv[...]
    charge = jnp.zeros(cls.shape, F32)
    for c in range(NCLS):
        charge = jnp.where(cls == c, jnp.broadcast_to(ccv[0:1, c : c + 1], cls.shape), charge)
    pbuf[0:3, 0:ls] = posv[...]
    pbuf[3:4, 0:ls] = charge
    x = pbuf[0:3]
    x = x - jnp.round(x)
    q = pbuf[3:4]
    x1 = x.astype(BF16).astype(F32)
    x2 = (x - x1).astype(BF16).astype(F32)
    x3 = x - x1 - x2
    half = jnp.where(q < 0.0, 0.5, 0.0)
    qc = jnp.maximum(jnp.abs(q), TINY)
    al2 = jnp.sqrt(qc)
    al = jnp.sqrt(al2)
    rows = jnp.concatenate(
        [x1, x2, x3, half, jnp.zeros((6, 128), F32), al2, al * A0, al * A1, al * A2,
         jnp.zeros((108, 128), F32)], axis=0
    )
    cols = rows.T
    own = lax.broadcasted_iota(jnp.int32, (1, 128), 1) < ls
    qown = jnp.where(own, qc, 0.0)
    tail = jnp.concatenate(
        [qown, jnp.where(own, jnp.abs(q) / qc, 0.0),
         jnp.broadcast_to(jnp.sum(qown, axis=1, keepdims=True), (1, 128)),
         jnp.zeros((5, 128), F32)], axis=0
    )
    ag_out[0:ls] = cols[0:ls]
    ag_out[ls:] = tail
    ag_in[si] = ag_out[...]

    @pl.when(si + ki > 0)
    def _():
        pl.semaphore_wait(barrier, si + ki)

    def ag_copy(src, to):
        return pltpu.make_async_remote_copy(
            src_ref=ag_out, dst_ref=ag_in.at[src], send_sem=ag_send.at[to],
            recv_sem=ag_recv.at[src], device_id=(to, ki), device_id_type=MESH,
        )

    @pl.loop(0, si)
    def _(s):
        tell(ready.at[si], s, ki)
        ag_copy(si, s).start()

    @pl.loop(0, ki)
    def _(k):
        tell(kin, si, k)

    mil_copy.wait()

    @pl.loop(0, n * (kb // KBW))
    def _(b):
        at = pl.ds(pl.multiple_of(b * KBW, KBW), KBW)
        m = mi[:, pl.ds(pl.multiple_of(shift * kb + b * KBW, KBW), KBW)].astype(F32)
        sq = jnp.sum(m * m, axis=0, keepdims=True)
        limit = float(MMAX * MMAX)
        wts[:, at] = limit * jnp.exp(sq * (-1.0 / limit)) / sq
        m16[:, at] = jnp.concatenate(
            [m, m, m, jnp.ones((1, KBW), F32), jnp.zeros((6, KBW), F32)], axis=0
        ).astype(BF16)

    def source(i):
        if nsite & (nsite - 1):
            return lax.rem(si + i, nsite)
        out, bit = 0, 1
        while bit < nsite:
            out = out + bit * lax.rem(lax.div(si, bit) + lax.div(i, bit), 2)
            bit *= 2
        return out

    def prepare(i):
        src = source(i)
        slot = lax.rem(i, 2)
        xs[slot] = ag_in[src, 0:ls, 0:16].astype(BF16)
        for c in range(4):
            co[slot, c] = jnp.broadcast_to(ag_in[src, 0:ls, 16 + c : 17 + c], (ls, 128))
        both = ag_in[src, ls : ls + 8]
        if nsites > 128:
            both = jnp.concatenate([both, jnp.zeros((8, nsites - 128), F32)], axis=1)
        qrow[...] += pltpu.roll(both, src * ls, 1)
        qtot[...] += ag_in[src, ls + 2 : ls + 3]

    def block_of(b):
        return pl.ds(pl.multiple_of(b * kb, kb), kb)

    prepare(0)
    tbuf[...] = jnp.dot(xs[0], m16[:, 0:kb], preferred_element_type=F32)

    @pl.loop(0, nsite)
    def _(i):
        src = source(i)
        slot = lax.rem(i, 2)

        @pl.loop(0, n)
        def _(b):
            last = lax.div(b + 1, n)

            @pl.when((last == 1) & (i < nsite - 1))
            def _():
                to = si + i + 2 - lax.div(1, i + 1)
                for o in range(2):
                    @pl.when((lax.rem(i, 2) + lax.div(1, i + 1) > 0) & (to + o < nsite))
                    def _():
                        pl.semaphore_wait(ready.at[to + o], 1)
                        ag_copy(si, to + o).start()

                nxt = source(i + 1)
                ag_copy(nxt, nxt).wait_recv()
                prepare(i + 1)

            turns = jnp.dot(
                xs[lax.rem(i + last, 2)], m16[:, block_of(b + 1 - last * n)],
                preferred_element_type=F32,
            )
            c0, c1, c2, c3 = co[slot, 0], co[slot, 1], co[slot, 2], co[slot, 3]
            for l in range(kb // 128):
                ln = slice(l * 128, (l + 1) * 128)
                at = pl.ds(pl.multiple_of(b * kb + l * 128, 128), 128)
                t = tbuf[:, ln]
                r = t - jnp.round(t)
                z = r * r
                s = r * (c1 + z * (c2 + z * c3))
                s2 = s * s
                u = c0 - s2
                sc = s * (u * lax.rsqrt(u))
                dc = u - s2
                sj = sc * dc
                cj = sc * sc
                psin[src, :, at] = sj
                pcos[src, :, at] = cj
                tbuf[:, ln] = turns[:, ln]
                sums, sumc = sj[0:8], cj[0:8]
                for g in range(1, ls // 8):
                    sums = sums + sj[8 * g : 8 * g + 8]
                    sumc = sumc + cj[8 * g : 8 * g + 8]
                ssin[:, at] += sums
                scos[:, at] += sumc

    @pl.when(ki < nka - 1)
    def _():
        pl.semaphore_wait(kin, nka - 1 - ki)

    @pl.loop(1, nka)
    def _(i):
        tell(kall, si, lax.rem(ki + i, nka))

    isn = 1.0 / math.sqrt(nsites)
    steps = n

    def step_of(j):
        return pl.ds(pl.multiple_of(j * kb, kb), kb)

    def weigh(j, counts):
        at = step_of(j)
        cimag = (4.0 * isn) * jnp.sum(ssin[:, at], axis=0, keepdims=True)
        total = jnp.concatenate([qtot[...]] * (kb // 128), axis=1)
        creal = isn * (total - 8.0 * jnp.sum(scos[:, at], axis=0, keepdims=True))
        w = wts[:, at]
        g1 = w * creal
        g2 = w * cimag
        e = g1 * creal + g2 * cimag
        eacc[...] += e if counts is None else jnp.where(counts, e, 0.0)
        g1v[...] = g1
        g2v[...] = 2.0 * g2

    weigh(0, None)

    @pl.loop(0, steps)
    def _(j):
        at = step_of(j)
        v = (psin[:, :, at] * g1v[...] + pcos[:, :, at] * g2v[...]).reshape(nsites, kb)
        hi = v.astype(BF16)
        lo = (v - hi.astype(F32)).astype(BF16)
        m = m16[:, at]
        dims = (((1,), (1,)), ((), ()))
        facc[...] += lax.dot_general(m, hi, dims, preferred_element_type=F32) + lax.dot_general(
            m, lo, dims, preferred_element_type=F32
        )
        weigh(jnp.minimum(j + 1, steps - 1), j + 1 < steps)

    en = eacc[:, 0:128]
    for l in range(1, kb // 128):
        en = en + eacc[:, l * 128 : (l + 1) * 128]
    if nsites > 128:
        en = jnp.concatenate([en, jnp.zeros((1, nsites - 128), F32)], axis=1)
    rs_out[...] = jnp.concatenate([facc[0:3], en], axis=0)

    pl.semaphore_wait(kall, nka - 1)

    def rs_copy(to):
        return pltpu.make_async_remote_copy(
            src_ref=rs_out, dst_ref=rs_in.at[me], send_sem=rs_send, recv_sem=rs_recv,
            device_id=(lax.div(to, nka), lax.rem(to, nka)), device_id_type=MESH,
        )

    @pl.loop(0, ndev)
    def _(to):
        @pl.when(to != me)
        def _():
            rs_copy(to).start()

    rs_in[me] = rs_out[...]
    others = rs_in.at[pl.ds(0, ndev - 1)]
    pltpu.make_async_copy(others, others, rs_recv).wait()

    total = jnp.sum(rs_in[...], axis=0)
    fall = total[0:3]
    qall, ratio = qrow[0:1], qrow[1:2]
    fscale = 16.0 * math.pi / math.sqrt(nsites * kvecs)
    mean = jnp.sum(fall, axis=1, keepdims=True) / jnp.sum(qall, axis=1, keepdims=True)
    forces = (fscale * ratio) * (fall - qall * mean)
    energy = jnp.sum(total[3:4], axis=1, keepdims=True) * (1.0 / kvecs)
    mine = pltpu.roll(
        jnp.concatenate([forces, jnp.zeros((5, nsites), F32)], axis=0), nsites - me * spd, 1
    )
    res_ref[...] = mine[:, 0:128]
    res_ref[3:4, :] = jnp.broadcast_to(energy, (1, 128))

    pltpu.make_async_copy(others, others, rs_send).wait()

    @pl.loop(1, nsite)
    def _(i):
        ag_copy(si, lax.rem(si + i, nsite)).wait_send()


def publish(res_ref, out_ref, en_ref):
    out_ref[...] = res_ref[0:3, 0 : out_ref.shape[1]]
    en_ref[...] = res_ref[3:4, 0:1]


def local(nsite, nka, positions, site_class, class_charge, miller):
    ndev = nsite * nka
    ls = positions.shape[1]
    nsites = ls * nsite
    kvecs = miller.shape[1] * nka
    spd = nsites // ndev
    kb = miller.shape[1] // (nsite * UNITS)
    span = shares(nsite, miller.shape[1] // kb)[1] * kb
    vmem = pl.BlockSpec(memory_space=pltpu.VMEM)
    summed = pl.pallas_call(
        functools.partial(kernel, nsite, nka, nsites, kvecs, kb),
        out_shape=pltpu.VMEM((8, 128), F32),
        in_specs=[pl.BlockSpec(memory_space=pl.ANY)] * 4,
        out_specs=vmem,
        scratch_shapes=[
            pltpu.VMEM((3, ls), F32),
            pltpu.VMEM((1, ls), jnp.int32),
            pltpu.VMEM((1, NCLS), F32),
            pltpu.VMEM((3, span), jnp.int32),
            pltpu.VMEM((16, span), BF16),
            pltpu.VMEM((1, span), F32),
            pltpu.VMEM((8, 128), F32),
            pltpu.VMEM((2, ls, 16), BF16),
            pltpu.VMEM((2, 4, ls, 128), F32),
            pltpu.VMEM((ls, kb), F32),
            pltpu.VMEM((nsite, ls, span), F32),
            pltpu.VMEM((nsite, ls, span), F32),
            pltpu.VMEM((8, span), F32),
            pltpu.VMEM((8, span), F32),
            pltpu.VMEM((8, nsites), F32),
            pltpu.VMEM((1, 128), F32),
            pltpu.VMEM((1, kb), F32),
            pltpu.VMEM((1, kb), F32),
            pltpu.VMEM((16, nsites), F32),
            pltpu.VMEM((1, kb), F32),
            pltpu.VMEM((ls + 8, 128), F32),
            pltpu.VMEM((nsite, ls + 8, 128), F32),
            pltpu.VMEM((4, nsites), F32),
            pltpu.VMEM((ndev, 4, nsites), F32),
            pltpu.SemaphoreType.DMA,
            pltpu.SemaphoreType.DMA,
            pltpu.SemaphoreType.DMA,
            pltpu.SemaphoreType.DMA,
            pltpu.SemaphoreType.DMA((nsite,)),
            pltpu.SemaphoreType.DMA((nsite,)),
            pltpu.SemaphoreType.DMA,
            pltpu.SemaphoreType.DMA,
            pltpu.SemaphoreType.REGULAR((nsite,)),
            pltpu.SemaphoreType.REGULAR,
            pltpu.SemaphoreType.REGULAR,
        ],
        compiler_params=pltpu.CompilerParams(collective_id=0, has_side_effects=True),
        name="ewald",
    )(positions, site_class.reshape(1, ls), class_charge.reshape(1, NCLS), miller)
    forces, energy = pl.pallas_call(
        publish,
        out_shape=(jax.ShapeDtypeStruct((3, spd), F32), jax.ShapeDtypeStruct((1, 1), F32)),
        in_specs=[vmem],
        out_specs=(vmem, vmem),
        name="publish",
    )(pltpu.with_memory_space_constraint(summed, pltpu.VMEM))
    return forces, energy[0, 0]


def solution(mesh):
    placed = (P(None, "site"), P("site"), P(), P(None, "ka"))
    return jax.shard_map(
        functools.partial(local, mesh.shape["site"], mesh.shape["ka"]),
        mesh=mesh,
        in_specs=placed,
        out_specs=(P(None, ("site", "ka")), P()),
        check_vma=False,
    )
```

time: 30.3 us -> 26.6 us (0.88)
  Pallas kernels: 29.5 us -> 25.8 us
    pallas_call x1, Pallas kernels: 28.9 us -> 25.2 us  [local(): pl.pallas_call(functools.partial(kernel, nsite, nka, nsites, kvecs, kb),...]
where the time goes in v2:
time: 26.6 us; the launch traced here: 26.5 us
  Pallas kernels  25.8 us (97%)
  between operations  0.64 us (2%)
    pallas_call x1, Pallas kernels, local(): pl.pallas_call(functools.partial(kernel, nsite, nka, nsites, kvecs, kb),...  25.2 us
    pallas_call x1, Pallas kernels, local(): pl.pallas_call(publish, out_shape=(jax.ShapeDtypeStruct((3, spd), F32), j...  0.58 us

profile of v2, /device:TPU:0, one launch (start us, length us, event | category | flops | bytes accessed | tf_op | source)
XLA Modules:
  0.0 26.5 jit_solution(15621904848203146031)
XLA Ops:
  0.6 25.2 %ewald.1.res_ref = f32[8,128]{1,0:T(8,128)S(1)} custom-call(f32[3,16]{1,0:T(4,128)} %pos_ref.1, s32[1,16]{1,0:T(1,128)} %bitcast.3, f32[1,4]{1,0:T(1,128)} %bitcast.4, s32[3,131072]{1,0:T(4,128)} %mil_ref.1), custom_call_target="tpu_custom_call" | custom-call | tf_op jit(solution)/shard_map/ewald/pallas_call | solution.py:331
  25.9 0.6 %publish.1 = (f32[3,4]{1,0:T(4,128)}, f32[1,1]{1,0:T(1,128)}) custom-call(f32[8,128]{1,0:T(8,128)S(1)} %ewald.1.res_ref), custom_call_target="tpu_custom_call" | custom-call | tf_op jit(solution)/shard_map/publish/pallas_call | solution.py:376

commit v3 on v2

--- a/solution.py
+++ b/solution.py
@@ -16,7 +16,8 @@
 A0, A1, A2 = 1.5707884689227576, -0.645711988911062, 0.07766738858001387
 TINY = 1e-24
 UNITS = 4
-SKEW = (1, 0)
+SKEW = (28, 8)
+OFFER = (2, 2)
 KBW = 1024
 
 
@@ -27,7 +28,8 @@
     def first(s):
         return units * s * (total - top * s) // span
 
-    return first, max(first(s + 1) - first(s) for s in range(nsite))
+    sizes = [first(s + 1) - first(s) for s in range(nsite)]
+    return first, max(sizes), min(sizes)
 
 
 def kernel(
@@ -45,7 +47,8 @@
     ls = posv.shape[1]
     spd = nsites // ndev
     units = mil_ref.shape[1] // kb
-    first, most = shares(nsite, units)
+    first, most, least = shares(nsite, units)
+    offers = [min(OFFER[0] + OFFER[1] * p, nsite * least - 1) for p in range(nsite // 2)]
     low = first(si)
     n = first(si + 1) - low
     base = jnp.minimum(low, units - most)
@@ -75,12 +78,6 @@
     def _(k):
         tell(barrier, si, k)
 
-    ssin[...] = jnp.zeros_like(ssin)
-    scos[...] = jnp.zeros_like(scos)
-    qrow[...] = jnp.zeros_like(qrow)
-    qtot[...] = jnp.zeros_like(qtot)
-    facc[...] = jnp.zeros_like(facc)
-    eacc[...] = jnp.zeros_like(eacc)
     pbuf[...] = jnp.zeros_like(pbuf)
 
     pos_copy.wait()
@@ -137,6 +134,12 @@
     def _(k):
         tell(kin, si, k)
 
+    ssin[...] = jnp.zeros_like(ssin)
+    scos[...] = jnp.zeros_like(scos)
+    qrow[...] = jnp.zeros_like(qrow)
+    qtot[...] = jnp.zeros_like(qtot)
+    facc[...] = jnp.zeros_like(facc)
+    eacc[...] = jnp.zeros_like(eacc)
     mil_copy.wait()
 
     @pl.loop(0, n * (kb // KBW))
@@ -177,55 +180,60 @@
     prepare(0)
     tbuf[...] = jnp.dot(xs[0], m16[:, 0:kb], preferred_element_type=F32)
 
+    def turn(i, b, slot, at_next):
+        src = source(i)
+        mine = lax.rem(i, 2)
+        turns = jnp.dot(xs[slot], m16[:, at_next], preferred_element_type=F32)
+        c0, c1, c2, c3 = co[mine, 0], co[mine, 1], co[mine, 2], co[mine, 3]
+        for l in range(kb // 128):
+            ln = slice(l * 128, (l + 1) * 128)
+            at = pl.ds(pl.multiple_of(b * kb + l * 128, 128), 128)
+            t = tbuf[:, ln]
+            r = t - jnp.round(t)
+            z = r * r
+            s = r * (c1 + z * (c2 + z * c3))
+            s2 = s * s
+            u = c0 - s2
+            sc = s * (u * lax.rsqrt(u))
+            dc = u - s2
+            sj = sc * dc
+            cj = sc * sc
+            psin[src, :, at] = sj
+            pcos[src, :, at] = cj
+            tbuf[:, ln] = turns[:, ln]
+            sums, sumc = sj[0:8], cj[0:8]
+            for g in range(1, ls // 8):
+                sums = sums + sj[8 * g : 8 * g + 8]
+                sumc = sumc + cj[8 * g : 8 * g + 8]
+            ssin[:, at] += sums
+            scos[:, at] += sumc
+
+    def offer(g):
+        for p, when in enumerate(offers):
+            @pl.when(g == when)
+            def _():
+                for o in (2 * p + 1, 2 * p + 2):
+                    @pl.when(si + o < nsite)
+                    def _():
+                        pl.semaphore_wait(ready.at[si + o], 1)
+                        ag_copy(si, si + o).start()
+
     @pl.loop(0, nsite)
     def _(i):
-        src = source(i)
-        slot = lax.rem(i, 2)
-
-        @pl.loop(0, n)
+        @pl.loop(0, n - 1)
         def _(b):
-            last = lax.div(b + 1, n)
-
-            @pl.when((last == 1) & (i < nsite - 1))
-            def _():
-                to = si + i + 2 - lax.div(1, i + 1)
-                for o in range(2):
-                    @pl.when((lax.rem(i, 2) + lax.div(1, i + 1) > 0) & (to + o < nsite))
-                    def _():
-                        pl.semaphore_wait(ready.at[to + o], 1)
-                        ag_copy(si, to + o).start()
-
-                nxt = source(i + 1)
-                ag_copy(nxt, nxt).wait_recv()
-                prepare(i + 1)
-
-            turns = jnp.dot(
-                xs[lax.rem(i + last, 2)], m16[:, block_of(b + 1 - last * n)],
-                preferred_element_type=F32,
-            )
-            c0, c1, c2, c3 = co[slot, 0], co[slot, 1], co[slot, 2], co[slot, 3]
-            for l in range(kb // 128):
-                ln = slice(l * 128, (l + 1) * 128)
-                at = pl.ds(pl.multiple_of(b * kb + l * 128, 128), 128)
-                t = tbuf[:, ln]
-                r = t - jnp.round(t)
-                z = r * r
-                s = r * (c1 + z * (c2 + z * c3))
-                s2 = s * s
-                u = c0 - s2
-                sc = s * (u * lax.rsqrt(u))
-                dc = u - s2
-                sj = sc * dc
-                cj = sc * sc
-                psin[src, :, at] = sj
-                pcos[src, :, at] = cj
-                tbuf[:, ln] = turns[:, ln]
-                sums, sumc = sj[0:8], cj[0:8]
-                for g in range(1, ls // 8):
-                    sums = sums + sj[8 * g : 8 * g + 8]
-                    sumc = sumc + cj[8 * g : 8 * g + 8]
-                ssin[:, at] += sums
-                scos[:, at] += sumc
+            offer(i * n + b)
+            turn(i, b, lax.rem(i, 2), block_of(b + 1))
+
+        offer(i * n + n - 1)
+
+        @pl.when(i < nsite - 1)
+        def _():
+            nxt = source(i + 1)
+            ag_copy(nxt, nxt).wait_recv()
+            prepare(i + 1)
+
+        turn(i, n - 1, lax.rem(i + 1, 2), block_of(0))
 
     @pl.when(ki < nka - 1)
     def _():
@@ -264,9 +272,10 @@
         lo = (v - hi.astype(F32)).astype(BF16)
         m = m16[:, at]
         dims = (((1,), (1,)), ((), ()))
-        facc[...] += lax.dot_general(m, hi, dims, preferred_element_type=F32) + lax.dot_general(
-            m, lo, dims, preferred_element_type=F32
+        both = lax.dot_general(
+            m, jnp.concatenate([hi, lo], axis=0), dims, preferred_element_type=F32
         )
+        facc[...] += both[:, 0:nsites] + both[:, nsites:]
         weigh(jnp.minimum(j + 1, steps - 1), j + 1 < steps)
 
     en = eacc[:, 0:128]

time: 26.6 us -> 24.8 us (0.932)
  Pallas kernels: 25.8 us -> 24 us
    pallas_call x1, Pallas kernels: 25.2 us -> 23.4 us  [local(): pl.pallas_call(functools.partial(kernel, nsite, nka, nsites, kvecs, kb),...]
where the time goes in v3:
time: 24.8 us; the launch traced here: 24.6 us
  Pallas kernels  24 us (97%)
  between operations  0.64 us (3%)
    pallas_call x1, Pallas kernels, local(): pl.pallas_call(functools.partial(kernel, nsite, nka, nsites, kvecs, kb),...  23.4 us
    pallas_call x1, Pallas kernels, local(): pl.pallas_call(publish, out_shape=(jax.ShapeDtypeStruct((3, spd), F32), j...  0.58 us

profile of v3, /device:TPU:0, one launch (start us, length us, event | category | flops | bytes accessed | tf_op | source)
XLA Modules:
  0.0 24.6 jit_solution(14714961339187019441)
XLA Ops:
  0.6 23.4 %ewald.1.res_ref = f32[8,128]{1,0:T(8,128)S(1)} custom-call(f32[3,16]{1,0:T(4,128)} %pos_ref.1, s32[1,16]{1,0:T(1,128)} %bitcast.3, f32[1,4]{1,0:T(1,128)} %bitcast.4, s32[3,131072]{1,0:T(4,128)} %mil_ref.1), custom_call_target="tpu_custom_call" | custom-call | tf_op jit(solution)/shard_map/ewald/pallas_call | solution.py:340
  24.1 0.6 %publish.1 = (f32[3,4]{1,0:T(4,128)}, f32[1,1]{1,0:T(1,128)}) custom-call(f32[8,128]{1,0:T(8,128)S(1)} %ewald.1.res_ref), custom_call_target="tpu_custom_call" | custom-call | tf_op jit(solution)/shard_map/publish/pallas_call | solution.py:385

commit v4 on v3

--- a/solution.py
+++ b/solution.py
@@ -16,9 +16,9 @@
 A0, A1, A2 = 1.5707884689227576, -0.645711988911062, 0.07766738858001387
 TINY = 1e-24
 UNITS = 4
-SKEW = (28, 8)
-OFFER = (2, 2)
-KBW = 1024
+SKEW = (36, 8)
+OFFER = (1, 3)
+WIDE = 4096
 
 
 def shares(nsite, units):
@@ -121,7 +121,7 @@
 
     def ag_copy(src, to):
         return pltpu.make_async_remote_copy(
-            src_ref=ag_out, dst_ref=ag_in.at[src], send_sem=ag_send.at[to],
+            src_ref=ag_out, dst_ref=ag_in.at[src], send_sem=ag_send,
             recv_sem=ag_recv.at[src], device_id=(to, ki), device_id_type=MESH,
         )
 
@@ -142,15 +142,17 @@
     eacc[...] = jnp.zeros_like(eacc)
     mil_copy.wait()
 
-    @pl.loop(0, n * (kb // KBW))
+    kbw = min(WIDE, kb)
+
+    @pl.loop(0, n * (kb // kbw))
     def _(b):
-        at = pl.ds(pl.multiple_of(b * KBW, KBW), KBW)
-        m = mi[:, pl.ds(pl.multiple_of(shift * kb + b * KBW, KBW), KBW)].astype(F32)
+        at = pl.ds(pl.multiple_of(b * kbw, kbw), kbw)
+        m = mi[:, pl.ds(pl.multiple_of(shift * kb + b * kbw, kbw), kbw)].astype(F32)
         sq = jnp.sum(m * m, axis=0, keepdims=True)
         limit = float(MMAX * MMAX)
         wts[:, at] = limit * jnp.exp(sq * (-1.0 / limit)) / sq
         m16[:, at] = jnp.concatenate(
-            [m, m, m, jnp.ones((1, KBW), F32), jnp.zeros((6, KBW), F32)], axis=0
+            [m, m, m, jnp.ones((1, kbw), F32), jnp.zeros((6, kbw), F32)], axis=0
         ).astype(BF16)
 
     def source(i):
@@ -243,6 +245,9 @@
     def _(i):
         tell(kall, si, lax.rem(ki + i, nka))
 
+    sent = ag_in.at[pl.ds(0, nsite - 1)]
+    pltpu.make_async_copy(sent, sent, ag_send).wait()
+
     isn = 1.0 / math.sqrt(nsites)
     steps = n
 
@@ -317,10 +322,6 @@
     res_ref[3:4, :] = jnp.broadcast_to(energy, (1, 128))
 
     pltpu.make_async_copy(others, others, rs_send).wait()
-
-    @pl.loop(1, nsite)
-    def _(i):
-        ag_copy(si, lax.rem(si + i, nsite)).wait_send()
 
 
 def publish(res_ref, out_ref, en_ref):
@@ -371,7 +372,7 @@
             pltpu.SemaphoreType.DMA,
             pltpu.SemaphoreType.DMA,
             pltpu.SemaphoreType.DMA,
-            pltpu.SemaphoreType.DMA((nsite,)),
+            pltpu.SemaphoreType.DMA,
             pltpu.SemaphoreType.DMA((nsite,)),
             pltpu.SemaphoreType.DMA,
             pltpu.SemaphoreType.DMA,

time: 24.8 us -> 24.3 us (0.980)
  Pallas kernels: 24 us -> 23.5 us
    pallas_call x1, Pallas kernels: 23.4 us -> 22.9 us  [local(): pl.pallas_call(functools.partial(kernel, nsite, nka, nsites, kvecs, kb),...]
where the time goes in v4:
time: 24.3 us; the launch traced here: 24.1 us
  Pallas kernels  23.5 us (97%)
  between operations  0.64 us (3%)
    pallas_call x1, Pallas kernels, local(): pl.pallas_call(functools.partial(kernel, nsite, nka, nsites, kvecs, kb),...  22.9 us
    pallas_call x1, Pallas kernels, local(): pl.pallas_call(publish, out_shape=(jax.ShapeDtypeStruct((3, spd), F32), j...  0.58 us

profile of v4, /device:TPU:0, one launch (start us, length us, event | category | flops | bytes accessed | tf_op | source)
XLA Modules:
  0.0 24.1 jit_solution(13183056242771811702)
XLA Ops:
  0.6 22.9 %ewald.1.res_ref = f32[8,128]{1,0:T(8,128)S(1)} custom-call(f32[3,16]{1,0:T(4,128)} %pos_ref.1, s32[1,16]{1,0:T(1,128)} %bitcast.3, f32[1,4]{1,0:T(1,128)} %bitcast.4, s32[3,131072]{1,0:T(4,128)} %mil_ref.1), custom_call_target="tpu_custom_call" | custom-call | tf_op jit(solution)/shard_map/ewald/pallas_call | solution.py:341
  23.5 0.6 %publish.1 = (f32[3,4]{1,0:T(4,128)}, f32[1,1]{1,0:T(1,128)}) custom-call(f32[8,128]{1,0:T(8,128)S(1)} %ewald.1.res_ref), custom_call_target="tpu_custom_call" | custom-call | tf_op jit(solution)/shard_map/publish/pallas_call | solution.py:386

commit v5 on v4

--- a/solution.py
+++ b/solution.py
@@ -211,14 +211,16 @@
             scos[:, at] += sumc
 
     def offer(g):
-        for p, when in enumerate(offers):
-            @pl.when(g == when)
-            def _():
-                for o in (2 * p + 1, 2 * p + 2):
-                    @pl.when(si + o < nsite)
-                    def _():
-                        pl.semaphore_wait(ready.at[si + o], 1)
-                        ag_copy(si, si + o).start()
+        @pl.when(g <= max(offers))
+        def _():
+            for p, when in enumerate(offers):
+                @pl.when(g == when)
+                def _():
+                    for o in (2 * p + 1, 2 * p + 2):
+                        @pl.when(si + o < nsite)
+                        def _():
+                            pl.semaphore_wait(ready.at[si + o], 1)
+                            ag_copy(si, si + o).start()
 
     @pl.loop(0, nsite)
     def _(i):

time: 24.3 us -> 23.8 us (0.979)
  Pallas kernels: 23.5 us -> 23 us
    pallas_call x1, Pallas kernels: 22.9 us -> 22.4 us  [local(): pl.pallas_call(functools.partial(kernel, nsite, nka, nsites, kvecs, kb),...]
where the time goes in v5:
time: 23.8 us; the launch traced here: 23.7 us
  Pallas kernels  23 us (97%)
  between operations  0.64 us (3%)
    pallas_call x1, Pallas kernels, local(): pl.pallas_call(functools.partial(kernel, nsite, nka, nsites, kvecs, kb),...  22.4 us
    pallas_call x1, Pallas kernels, local(): pl.pallas_call(publish, out_shape=(jax.ShapeDtypeStruct((3, spd), F32), j...  0.58 us

profile of v5, /device:TPU:0, one launch (start us, length us, event | category | flops | bytes accessed | tf_op | source)
XLA Modules:
  0.0 23.7 jit_solution(12774120323229214546)
XLA Ops:
  0.6 22.4 %ewald.1.res_ref = f32[8,128]{1,0:T(8,128)S(1)} custom-call(f32[3,16]{1,0:T(4,128)} %pos_ref.1, s32[1,16]{1,0:T(1,128)} %bitcast.3, f32[1,4]{1,0:T(1,128)} %bitcast.4, s32[3,131072]{1,0:T(4,128)} %mil_ref.1), custom_call_target="tpu_custom_call" | custom-call | tf_op jit(solution)/shard_map/ewald/pallas_call | solution.py:343
  23.1 0.6 %publish.1 = (f32[3,4]{1,0:T(4,128)}, f32[1,1]{1,0:T(1,128)}) custom-call(f32[8,128]{1,0:T(8,128)S(1)} %ewald.1.res_ref), custom_call_target="tpu_custom_call" | custom-call | tf_op jit(solution)/shard_map/publish/pallas_call | solution.py:388
